TPU v7x, 32 devices: a whole 2x2x4 slice. The times are simulated.
32 devices in a mesh: dp: 4 (over y, x), expert: 8 (over z, core).
Axes of the slice: x: 2, y: 2, z: 4, core: 2. Of those that a mesh axis runs over, the one named last changes fastest.
Arguments:
- hidden: bfloat16 [8, 4608, 1408], P('expert', 'dp')
- upstream: bfloat16 [8, 4608, 2048], P('expert', 'dp')
- token_counts: int32 [8, 4], P('expert', 'dp'), may hold values from 1 to 1152, as said below
- master: float32 [8, 1408, 2048], P('expert', 'dp'), may hold values from -0.15625 to 0.15625
- first_moment: float32 [8, 1408, 2048], P('expert', 'dp'), may hold values from -6 to 6
- second_moment: float32 [8, 1408, 2048], P('expert', 'dp'), may hold values from 0.25 to 4
- router_input: bfloat16 [4096, 2048], P(('dp', 'expert')), may hold values from -6 to 6
- router_cot: bfloat16 [64, 4096], P(None, ('dp', 'expert'))
- router_master: float32 [64, 2048], replicated, may hold values from -0.125 to 0.125
- router_first: float32 [64, 2048], replicated, may hold values from -6 to 6
- router_second: float32 [64, 2048], replicated, may hold values from 0.25 to 4
- partner: int32 [8], replicated, may hold values from 0 to 7, as said below
Outputs:
- new_weight: bfloat16 [8, 1408, 2048], P('expert')
- new_master: float32 [8, 1408, 2048], P('expert', 'dp')
- new_first: float32 [8, 1408, 2048], P('expert', 'dp')
- new_second: float32 [8, 1408, 2048], P('expert', 'dp')
- router_master_new: float32 [64, 2048], replicated
- router_first_new: float32 [64, 2048], replicated
- router_second_new: float32 [64, 2048], replicated
Inputs may be any that keep to these rules, and one draw needn't show every extreme that they name: partner[partner[p]] = p for every position p; a position with partner[p] = p keeps its expert. The first token_counts[e, d] of replica d's 1152 slots for position e are live, the rest are padding.
All inputs are finite; a program needn't handle non-finite values.
Results may differ from a plain program's by a relative error of at most 0.001.
Values may be sent and summed in bfloat16 or wider, within the bound.
A program may use at most 128 MiB of HBM per device.

v0:
```python
import math
import jax
import jax.numpy as jnp
from jax import lax
from jax.sharding import PartitionSpec as P

beta_first = 0.9
beta_second = 0.95
learn_rate = 0.001
decay_weight = 0.1
adam_eps = 1e-08
norm_eps = 1e-06
correct_first = 1.0 - 0.9**10
correct_second = 1.0 - 0.95**10


def adam_update(gradient, moment_one, moment_two, weights):
    first_new = beta_first * moment_one + (1.0 - beta_first) * gradient
    second_new = beta_second * moment_two + (1.0 - beta_second) * gradient * gradient
    ratio = first_new / correct_first / (jnp.sqrt(second_new / correct_second) + adam_eps)
    weights_new = weights - learn_rate * (ratio + decay_weight * weights)
    return (weights_new, first_new, second_new)


code_top = 32767.0
steps_per_octave = 256.0


def scale_of(level):
    return jnp.exp2(level.astype(jnp.float32) * (1.0 / steps_per_octave))


def encode(blocks):
    groups, rows, width = blocks.shape
    peak = jnp.maximum(jnp.max(jnp.abs(blocks), axis=2), 1e-37)
    level = jnp.clip(jnp.ceil(jnp.log2(peak) * steps_per_octave), -32000.0, 32767.0).astype(
        jnp.int16
    )
    scaled = blocks * (code_top / scale_of(level))[:, :, None]
    codes = jnp.clip(jnp.round(scaled), -code_top, code_top).astype(jnp.int16)
    extra = -(-rows // width)
    levels = jnp.pad(level, ((0, 0), (0, extra * width - rows))).reshape(groups, extra, width)
    return jnp.concatenate([codes, levels], axis=1)


def decode(payload, rows):
    groups, _, width = payload.shape
    level = payload[:, rows:].reshape(groups, -1)[:, :rows]
    return payload[:, :rows].astype(jnp.float32) * (scale_of(level) * (1.0 / code_top))[:, :, None]


def to_pieces(matrix, groups):
    rows, width = matrix.shape
    return matrix.reshape(rows, groups, width // groups).swapaxes(0, 1)


def from_pieces(pieces):
    groups, rows, width = pieces.shape
    return pieces.swapaxes(0, 1).reshape(rows, groups * width)


def exchange(payload, axis="expert"):
    return lax.all_to_all(payload, axis, split_axis=0, concat_axis=0, tiled=True)


def regather(weight_shard):
    return lax.all_gather(weight_shard, "dp", axis=0, tiled=True)


def on_device(
    hidden,
    upstream,
    token_counts,
    master,
    first_moment,
    second_moment,
    router_input,
    router_cot,
    router_master,
    router_first,
    router_second,
    partner,
):
    hidden_units = hidden.shape[2]
    features = upstream.shape[2]
    row_count = hidden.shape[1]
    groups = lax.axis_size("expert")
    rows = master.shape[1]
    early_master = exchange(encode(to_pieces(master[0], groups)))
    early_first = exchange(encode(to_pieces(first_moment[0], groups)))
    early_second = exchange(encode(to_pieces(second_moment[0], groups)))
    live_rows = jnp.arange(row_count, dtype=jnp.int32) < token_counts[0, 0]
    activations = hidden[0]
    grads_out = upstream[0]
    masked_out = jnp.where(live_rows[:, None], grads_out, jnp.zeros_like(grads_out))
    router_partial = jnp.dot(router_cot, router_input, preferred_element_type=jnp.float32)
    partial = lax.dot_general(
        activations, masked_out, (((0,), (0,)), ((), ())), preferred_element_type=jnp.float32
    )
    gradient = lax.psum_scatter(partial, "dp", scatter_dimension=0, tiled=True)
    moved_gradient = exchange(encode(to_pieces(gradient, groups)))
    router_grad = lax.psum(router_partial, ("dp", "expert"))
    expert_square = lax.psum(jnp.sum(gradient * gradient), ("dp", "expert"))
    total_square = expert_square + jnp.sum(router_grad * router_grad)
    clip_limit = 2.0 * math.sqrt(
        float(groups * hidden_units * features + router_cot.shape[0] * features)
    )
    factor = jnp.minimum(1.0, clip_limit / (jnp.sqrt(total_square) + norm_eps))
    states = adam_update(
        factor * decode(moved_gradient, rows),
        decode(early_first, rows),
        decode(early_second, rows),
        decode(early_master, rows),
    )
    router_outs = adam_update(factor * router_grad, router_first, router_second, router_master)
    sent = [
        encode(jnp.take(member, partner, axis=0)) for member in (states[0], states[1], states[2])
    ]
    moved = [from_pieces(decode(exchange(payload), rows)) for payload in sent]
    moved_weight = regather(moved[0].astype(jnp.bfloat16))
    return (
        moved_weight[None],
        moved[0][None],
        moved[1][None],
        moved[2][None],
        router_outs[0],
        router_outs[1],
        router_outs[2],
    )


def solution(mesh):
    in_specs = (
        P("expert", "dp", None),
        P("expert", "dp", None),
        P("expert", "dp"),
        P("expert", "dp", None),
        P("expert", "dp", None),
        P("expert", "dp", None),
        P(("dp", "expert"), None),
        P(None, ("dp", "expert")),
        P(),
        P(),
        P(),
        P(),
    )
    out_specs = (
        P("expert", None, None),
        P("expert", "dp", None),
        P("expert", "dp", None),
        P("expert", "dp", None),
        P(),
        P(),
        P(),
    )
    return jax.shard_map(
        on_device, mesh=mesh, in_specs=in_specs, out_specs=out_specs, check_vma=False
    )
```

profile of v0, /device:TPU:0, one launch (start us, length us, event | category | flops | bytes accessed | tf_op | source)
XLA Modules:
  0.0 543.5 jit_solution(693130620030949028)
XLA Ops:
  9.9 12.9 %convolution_bitcast_fusion = f32[1408,2048]{0,1:T(8,128)} fusion(bf16[1,1152,2048]{2,1,0:T(8,128)(2,1)} %param.15, pred[1152]{0:T(1024)(128)(4,1)S(1)} %iota_compare_fusion, bf16[1,1152,1408]{2,1,0:T(8,128)(2,1)S(1)} %copy-done), kind=kOutput, calls=%fused_computation.3 | convolution fusion | flops 6646136832 | bytes 19498112 | tf_op jit(solution)/shard_map/dot_general | solution.py:97
  22.8 12.0 %copy.42 = f32[1408,2048]{1,0:T(8,128)} copy(f32[1408,2048]{0,1:T(8,128)} %convolution_bitcast_fusion) | data formatting | bytes 23068672
  41.4 6.4 %all-to-all-start.3 = ((s16[8,354,256]{2,1,0:T(8,128)(2,1)}), s16[8,354,256]{2,1,0:T(8,128)(2,1)}, u32[]{:S(2)}, u32[]{:S(2)}) async-start(s16[8,354,256]{2,1,0:T(8,128)(2,1)} %pad_add_fusion.3), calls=%async_computation.3 | async-start | bytes 2949120 | tf_op jit(solution)/shard_map/all_to_all | solution.py:63
  54.2 29.3 %all-to-all-done.3 = s16[8,354,256]{2,1,0:T(8,128)(2,1)} async-done(((s16[8,354,256]{2,1,0:T(8,128)(2,1)}), s16[8,354,256]{2,1,0:T(8,128)(2,1)}, u32[]{:S(2)}, u32[]{:S(2)}) %all-to-all-start.3) | async-done | bytes 1450016 | tf_op jit(solution)/shard_map/all_to_all | solution.py:63
  83.5 4.3 all-to-all-start.1
  94.3 29.2 %all-to-all-done.1 = s16[8,354,256]{2,1,0:T(8,128)(2,1)} async-done(((s16[8,354,256]{2,1,0:T(8,128)(2,1)}), s16[8,354,256]{2,1,0:T(8,128)(2,1)}, u32[]{:S(2)}, u32[]{:S(2)}) %all-to-all-start.1) | async-done | bytes 1450016 | tf_op jit(solution)/shard_map/all_to_all | solution.py:63
  123.5 4.3 all-to-all-start
  127.8 22.0 %reduce-scatter.4.cloned.1.call-done = f32[352,2048]{1,0:T(8,128)} async-done(((f32[1408,2048]{1,0:T(8,128)}), f32[352,2048]{1,0:T(8,128)}) %reduce-scatter.4.cloned.1.call-update) | async-done | bytes 2883600
  163.5 4.3 all-to-all-start.2
  170.0 141.4 %all-reduce.9.cloned.1.call-done = f32[64,2048]{1,0:T(8,128)} async-done(((f32[64,2048]{1,0:T(8,128)}), f32[64,2048]{1,0:T(8,128)}) %all-reduce.9.cloned.1.call-update) | async-done | bytes 524304 | tf_op jit(solution)/shard_map/psum | solution.py:102
  317.0 39.8 %psum.14 = f32[]{:T(128)} all-reduce(f32[]{:T(128)} %multiply_reduce_fusion), channel_id=1, replica_groups=mesh['dp'=4,'expert'=8] {'dp','expert'}, use_global_device_ids=true, to_apply=%region_4.5 | all-reduce | flops 1 | bytes 8 | tf_op jit(solution)/shard_map/psum | solution.py:103
  358.9 8.5 %multiply_subtract_fusion = (f32[8,352,256]{2,1,0:T(8,128)}, f32[8,352,256]{2,1,0:T(8,128)}, f32[8,352,256]{2,1,0:T(8,128)}) fusion(s16[8,354,256]{2,1,0:T(8,128)(2,1)} %all-to-all-done, f32[8,352]{1,0:T(8,128)S(1)} %exponential_multiply_fusion.6, f32[8,352]{1,0:T(8,128)S(1)} %exponential_multiply_fusion.4, s16[8,354,256]{2,1,0:T(8,128)(2,1)} %all-to-all-done.2, ...), kind=kLoop, calls=%fused_computation.44 | loop fusion | flops 17301504 | bytes 14462980 | tf_op jit(solution)/shard_map/sub | solution.py:21
  370.0 4.1 gather_fusion.1
  378.2 4.4 abs_reduce_fusion
  382.8 5.7 %clamp_convert_fusion = (s16[8,352,256]{2,1,0:T(8,128)(2,1)}, s16[8,352,256]{2,1,0:T(8,128)(2,1)}, s16[8,352,256]{2,1,0:T(8,128)(2,1)S(1)}) fusion(f32[8,352,256]{2,1,0:T(8,128)} %gather_fusion.2, f32[8,352]{1,0:T(8,128)S(1)} %get-tuple-element.14, pred[8]{0:T(512)(128)(4,1)S(1)} %compare_and_fusion, f32[8,352]{1,0:T(8,128)S(1)} %get-tuple-element.36, ...), kind=kLoop, calls=%fused_computation.36 | loop fusion | flops 10813440 | bytes 13009928 | tf_op jit(solution)/shard_map/convert_element_type | solution.py:40
  388.6 39.1 %all_to_all.35 = s16[8,354,256]{2,1,0:T(8,128)(2,1)S(1)} all-to-all(s16[8,354,256]{2,1,0:T(8,128)(2,1)S(1)} %pad_add_fusion.4), channel_id=1, replica_groups=mesh['dp'=4,'expert'=8] {'expert'}, dimensions={0} | all-to-all | bytes 2899968 | tf_op jit(solution)/shard_map/all_to_all | solution.py:63
  432.2 4.3 all-to-all-start.6
  439.3 32.9 %all-to-all-done.6 = s16[8,354,256]{2,1,0:T(8,128)(2,1)} async-done(((s16[8,354,256]{2,1,0:T(8,128)(2,1)}), s16[8,354,256]{2,1,0:T(8,128)(2,1)}, u32[]{:S(2)}, u32[]{:S(2)}) %all-to-all-start.6) | async-done | bytes 1450016 | tf_op jit(solution)/shard_map/all_to_all | solution.py:63
  472.3 4.6 all-to-all-start.5
  485.7 4.2 broadcast_in_dim_reshape.11
  489.8 22.4 %all-to-all-done.5 = s16[8,354,256]{2,1,0:T(8,128)(2,1)} async-done(((s16[8,354,256]{2,1,0:T(8,128)(2,1)}), s16[8,354,256]{2,1,0:T(8,128)(2,1)}, u32[]{:S(2)}, u32[]{:S(2)}) %all-to-all-start.5) | async-done | bytes 1450016 | tf_op jit(solution)/shard_map/all_to_all | solution.py:63
  518.2 4.2 broadcast_in_dim_reshape.10
  525.6 4.2 broadcast_in_dim_reshape.9
  529.8 6.3 %copy.64 = bf16[1,1408,2048]{2,1,0:T(8,128)(2,1)} copy(bf16[1,1408,2048]{2,1,0:T(8,128)(2,1)} %bitcast.107) | data formatting | bytes 11534336
  (95 shorter events, 74.9 us)
Async XLA Ops:
  8.0 1.9 copy-start
  8.0 141.7 %reduce-scatter.4.cloned.1.call-start = ((), (), s32[]{:S(2)}) async-start(), calls=%async_computation.10 | async-start | bytes 14417920
  41.4 42.2 %all-to-all-start.3 = ((s16[8,354,256]{2,1,0:T(8,128)(2,1)}), s16[8,354,256]{2,1,0:T(8,128)(2,1)}, u32[]{:S(2)}, u32[]{:S(2)}) async-start(s16[8,354,256]{2,1,0:T(8,128)(2,1)} %pad_add_fusion.3), calls=%async_computation.3 | async-start | bytes 2949120 | tf_op jit(solution)/shard_map/all_to_all | solution.py:63
  83.5 40.0 %all-to-all-start.1 = ((s16[8,354,256]{2,1,0:T(8,128)(2,1)}), s16[8,354,256]{2,1,0:T(8,128)(2,1)}, u32[]{:S(2)}, u32[]{:S(2)}) async-start(s16[8,354,256]{2,1,0:T(8,128)(2,1)} %pad_add_fusion.1), calls=%async_computation.1 | async-start | bytes 2949120 | tf_op jit(solution)/shard_map/all_to_all | solution.py:63
  123.5 40.0 %all-to-all-start = ((s16[8,354,256]{2,1,0:T(8,128)(2,1)}), s16[8,354,256]{2,1,0:T(8,128)(2,1)}, u32[]{:S(2)}, u32[]{:S(2)}) async-start(s16[8,354,256]{2,1,0:T(8,128)(2,1)} %pad_add_fusion), calls=%async_computation | async-start | bytes 2949120 | tf_op jit(solution)/shard_map/all_to_all | solution.py:63
  159.0 8.8 %copy-start.2 = (bf16[64,128]{1,0:T(8,128)(2,1)S(1)}, bf16[64,128]{1,0:T(8,128)(2,1)}, u32[]{:S(2)}) copy-start(bf16[64,128]{1,0:T(8,128)(2,1)} %param.21) | copy-start | bytes 49156
  160.2 9.8 %copy-start.3 = (s32[8]{0:T(128)S(1)}, s32[8]{0:T(128)}, u32[]{:S(2)}) copy-start(s32[8]{0:T(128)} %param.25) | copy-start | bytes 100
  163.5 194.7 %all-to-all-start.2 = ((s16[8,354,256]{2,1,0:T(8,128)(2,1)}), s16[8,354,256]{2,1,0:T(8,128)(2,1)}, u32[]{:S(2)}, u32[]{:S(2)}) async-start(s16[8,354,256]{2,1,0:T(8,128)(2,1)} %pad_add_fusion.2), calls=%async_computation.2 | async-start | bytes 2949120 | tf_op jit(solution)/shard_map/all_to_all | solution.py:63
  167.8 143.6 %all-reduce.9.cloned.1.call-start = ((), (), s32[]{:S(2)}) async-start(), calls=%async_computation.8 | async-start | bytes 1048576 | tf_op jit(solution)/shard_map/psum | solution.py:102
  169.9 359.8 %all-gather.2.cloned.1.call-start = ((), (), s32[]{:S(2)}) async-start(), calls=%async_computation.9 | async-start | bytes 7208960 | tf_op jit(solution)/shard_map/all_gather | solution.py:67
  432.2 40.0 %all-to-all-start.6 = ((s16[8,354,256]{2,1,0:T(8,128)(2,1)}), s16[8,354,256]{2,1,0:T(8,128)(2,1)}, u32[]{:S(2)}, u32[]{:S(2)}) async-start(s16[8,354,256]{2,1,0:T(8,128)(2,1)} %pad_add_fusion.6), calls=%async_computation.6 | async-start | bytes 2949120 | tf_op jit(solution)/shard_map/all_to_all | solution.py:63
  472.3 40.0 %all-to-all-start.5 = ((s16[8,354,256]{2,1,0:T(8,128)(2,1)}), s16[8,354,256]{2,1,0:T(8,128)(2,1)}, u32[]{:S(2)}, u32[]{:S(2)}) async-start(s16[8,354,256]{2,1,0:T(8,128)(2,1)} %pad_add_fusion.5), calls=%async_computation.5 | async-start | bytes 2949120 | tf_op jit(solution)/shard_map/all_to_all | solution.py:63
  529.8 6.3 %copy-start.1 = (bf16[1,1152,1408]{2,1,0:T(8,128)(2,1)S(1)}, bf16[1,1152,1408]{2,1,0:T(8,128)(2,1)}, u32[]{:S(2)}) copy-start(bf16[1,1152,1408]{2,1,0:T(8,128)(2,1)} %param.14) | copy-start | bytes 9732100
Sparse Core Ops, SparseCore 0:
  35.0 114.7 reduce-scatter.3
  429.8 64.6 all-gather.1
Sparse Core Ops, SparseCore 1:
  174.1 137.3 all-reduce.8
where the time goes:
time: 546 us; the launch traced here: 544 us
  waiting for transfers between devices  281 us (51%)
  blocking collectives  78.9 us (14%)
  local copies, waits for them, and re-layouts  72.4 us (13%)
  other arithmetic  50.5 us (9%)
  starting transfers between devices  28.2 us (5%)
  between operations  18 us (3%)
  matrix products  14.9 us (3%)
    psum x1, waiting for transfers between devices, on_device(): router_grad = lax.psum(router_partial, ('dp', 'expert'))  141 us
    all_to_all x6, waiting for transfers between devices, exchange(): lax.all_to_all(payload, axis, split_axis=0, concat_axis=0, tiled=True)  117 us
    psum x1, blocking collectives, on_device(): expert_square = lax.psum(jnp.sum(gradient * gradient), ('dp', 'expert'))  39.8 us
    all_to_all x1, blocking collectives, exchange(): lax.all_to_all(payload, axis, split_axis=0, concat_axis=0, tiled=True)  39.1 us
    unnamed x28, local copies, waits for them, and re-layouts  35.7 us
    all_to_all x6, starting transfers between devices, exchange(): lax.all_to_all(payload, axis, split_axis=0, concat_axis=0, tiled=True)  28.1 us
    unnamed x4, waiting for transfers between devices  22 us
    dot_general x1, matrix products, on_device(): lax.dot_general(activations, masked_out, (((0,), (0,)), ((), ())), prefer...  12.9 us
  transfers between devices with their start and end apart: 9, of which 7 were waited for; matrix products, arithmetic and copies ran while one was open for 13% of the time, Pallas kernels for 0%

commit v1 on v0

--- a/solution.py
+++ b/solution.py
@@ -99,7 +99,8 @@
     )
     gradient = lax.psum_scatter(partial, "dp", scatter_dimension=0, tiled=True)
     moved_gradient = exchange(encode(to_pieces(gradient, groups)))
-    router_grad = lax.psum(router_partial, ("dp", "expert"))
+    parts = lax.all_gather(router_partial, ("dp", "expert"), axis=0, tiled=False)
+    router_grad = parts.sum(axis=0)
     expert_square = lax.psum(jnp.sum(gradient * gradient), ("dp", "expert"))
     total_square = expert_square + jnp.sum(router_grad * router_grad)
     clip_limit = 2.0 * math.sqrt(

time: 546 us -> 485 us (0.89)
  waiting for transfers between devices: 281 us -> 202 us
  blocking collectives: 78.9 us -> 91.1 us
  other arithmetic: 50.5 us -> 56.3 us
    psum x1 -> x0, waiting for transfers between devices: 141 us -> none  [on_device(): router_grad = lax.psum(router_partial, ('dp', 'expert'))]
    all_to_all x6, waiting for transfers between devices: 117 us -> 159 us  [exchange(): lax.all_to_all(payload, axis, split_axis=0, concat_axis=0, tiled=True)]
    unnamed x4, waiting for transfers between devices: 22 us -> 42.1 us
    psum x1, blocking collectives: 39.8 us -> 52 us  [on_device(): expert_square = lax.psum(jnp.sum(gradient * gradient), ('dp', 'expert'))]
    reduce_sum x0 -> x1, other arithmetic: none -> 6.9 us  [on_device(): router_grad = parts.sum(axis=0)]
    unnamed x28 -> x32, local copies, waits for them, and re-layouts: 35.7 us -> 36.9 us
  transfers between devices with their start and end apart: 9 -> 9, of which waited for: 7 -> 6; matrix products, arithmetic and copies ran while one was open for 13% -> 15% of each run, Pallas kernels for 0% -> 0%
where the time goes in v1:
time: 485 us; the launch traced here: 483 us
  waiting for transfers between devices  202 us (42%)
  blocking collectives  91.1 us (19%)
  local copies, waits for them, and re-layouts  73.7 us (15%)
  other arithmetic  56.3 us (12%)
  starting transfers between devices  28.3 us (6%)
  between operations  18 us (4%)
  matrix products  13.9 us (3%)
    all_to_all x6, waiting for transfers between devices, exchange(): lax.all_to_all(payload, axis, split_axis=0, concat_axis=0, tiled=True)  159 us
    psum x1, blocking collectives, on_device(): expert_square = lax.psum(jnp.sum(gradient * gradient), ('dp', 'expert'))  52 us
    unnamed x4, waiting for transfers between devices  42.1 us
    all_to_all x1, blocking collectives, exchange(): lax.all_to_all(payload, axis, split_axis=0, concat_axis=0, tiled=True)  39.1 us
    unnamed x32, local copies, waits for them, and re-layouts  36.9 us
    all_to_all x6, starting transfers between devices, exchange(): lax.all_to_all(payload, axis, split_axis=0, concat_axis=0, tiled=True)  28.2 us
    dot_general x1, matrix products, on_device(): lax.dot_general(activations, masked_out, (((0,), (0,)), ((), ())), prefer...  12.9 us
    sub x2, other arithmetic, adam_update(): weights_new = weights - learn_rate * (ratio + decay_weight * weights)  11.4 us
  transfers between devices with their start and end apart: 9, of which 6 were waited for; matrix products, arithmetic and copies ran while one was open for 15% of the time, Pallas kernels for 0%

profile of v1, /device:TPU:0, one launch (start us, length us, event | category | flops | bytes accessed | tf_op | source)
XLA Modules:
  0.0 482.8 jit_solution(5101101022983816664)
XLA Ops:
  9.9 12.9 %convolution_bitcast_fusion = f32[1408,2048]{0,1:T(8,128)} fusion(bf16[1,1152,2048]{2,1,0:T(8,128)(2,1)} %param.15, pred[1152]{0:T(1024)(128)(4,1)S(1)} %iota_compare_fusion, bf16[1,1152,1408]{2,1,0:T(8,128)(2,1)S(1)} %copy-done), kind=kOutput, calls=%fused_computation.3 | convolution fusion | flops 6646136832 | bytes 19498112 | tf_op jit(solution)/shard_map/dot_general | solution.py:97
  22.9 12.0 %copy.42 = f32[1408,2048]{1,0:T(8,128)} copy(f32[1408,2048]{0,1:T(8,128)} %convolution_bitcast_fusion) | data formatting | bytes 23068672
  43.5 6.4 %all-to-all-start.3 = ((s16[8,354,256]{2,1,0:T(8,128)(2,1)}), s16[8,354,256]{2,1,0:T(8,128)(2,1)}, u32[]{:S(2)}, u32[]{:S(2)}) async-start(s16[8,354,256]{2,1,0:T(8,128)(2,1)} %pad_add_fusion.3), calls=%async_computation.3 | async-start | bytes 2949120 | tf_op jit(solution)/shard_map/all_to_all | solution.py:63
  56.5 40.4 %all-to-all-done.3 = s16[8,354,256]{2,1,0:T(8,128)(2,1)} async-done(((s16[8,354,256]{2,1,0:T(8,128)(2,1)}), s16[8,354,256]{2,1,0:T(8,128)(2,1)}, u32[]{:S(2)}, u32[]{:S(2)}) %all-to-all-start.3) | async-done | bytes 1450016 | tf_op jit(solution)/shard_map/all_to_all | solution.py:63
  96.8 4.3 all-to-all-start.1
  107.8 44.3 %all-to-all-done.1 = s16[8,354,256]{2,1,0:T(8,128)(2,1)} async-done(((s16[8,354,256]{2,1,0:T(8,128)(2,1)}), s16[8,354,256]{2,1,0:T(8,128)(2,1)}, u32[]{:S(2)}, u32[]{:S(2)}) %all-to-all-start.1) | async-done | bytes 1450016 | tf_op jit(solution)/shard_map/all_to_all | solution.py:63
  152.1 4.4 all-to-all-start
  156.5 42.0 %reduce-scatter.4.cloned.1.call-done = f32[352,2048]{1,0:T(8,128)} async-done(((f32[1408,2048]{1,0:T(8,128)}), f32[352,2048]{1,0:T(8,128)}) %reduce-scatter.4.cloned.1.call-update) | async-done | bytes 2883600
  209.0 19.3 %all-to-all-done = s16[8,354,256]{2,1,0:T(8,128)(2,1)} async-done(((s16[8,354,256]{2,1,0:T(8,128)(2,1)}), s16[8,354,256]{2,1,0:T(8,128)(2,1)}, u32[]{:S(2)}, u32[]{:S(2)}) %all-to-all-start) | async-done | bytes 1450016 | tf_op jit(solution)/shard_map/all_to_all | solution.py:63
  228.3 4.3 all-to-all-start.2
  236.5 52.0 %psum.7 = f32[]{:T(128)} all-reduce(f32[]{:T(128)} %multiply_reduce_fusion), channel_id=1, replica_groups=mesh['dp'=4,'expert'=8] {'dp','expert'}, use_global_device_ids=true, to_apply=%region_4.5 | all-reduce | flops 1 | bytes 8 | tf_op jit(solution)/shard_map/psum | solution.py:104
  289.3 6.9 %reduce_sum.28 = f32[64,2048]{1,0:T(8,128)S(1)} reduce(f32[32,64,2048]{2,1,0:T(8,128)} %bitcast.108, f32[]{:T(128)} %constant.81.clone.1), dimensions={0}, to_apply=%region_5.6 | reduce | flops 4063232 | bytes 17301508 | tf_op jit(solution)/shard_map/reduce_sum | solution.py:103
  298.3 8.5 %multiply_subtract_fusion = (f32[8,352,256]{2,1,0:T(8,128)}, f32[8,352,256]{2,1,0:T(8,128)}, f32[8,352,256]{2,1,0:T(8,128)}) fusion(s16[8,354,256]{2,1,0:T(8,128)(2,1)} %all-to-all-done, f32[8,352]{1,0:T(8,128)S(1)} %exponential_multiply_fusion.6, f32[8,352]{1,0:T(8,128)S(1)} %exponential_multiply_fusion.4, s16[8,354,256]{2,1,0:T(8,128)(2,1)} %all-to-all-done.2, ...), kind=kLoop, calls=%fused_computation.44 | loop fusion | flops 17301504 | bytes 14462980 | tf_op jit(solution)/shard_map/sub | solution.py:21
  317.6 4.4 abs_reduce_fusion
  322.1 5.7 %clamp_convert_fusion = (s16[8,352,256]{2,1,0:T(8,128)(2,1)}, s16[8,352,256]{2,1,0:T(8,128)(2,1)}, s16[8,352,256]{2,1,0:T(8,128)(2,1)S(1)}) fusion(f32[8,352,256]{2,1,0:T(8,128)} %gather_fusion.2, f32[8,352]{1,0:T(8,128)S(1)} %get-tuple-element.14, pred[8]{0:T(512)(128)(4,1)S(1)} %compare_and_fusion, f32[8,352]{1,0:T(8,128)S(1)} %get-tuple-element.36, ...), kind=kLoop, calls=%fused_computation.36 | loop fusion | flops 10813440 | bytes 13009928 | tf_op jit(solution)/shard_map/convert_element_type | solution.py:40
  327.9 39.1 %all_to_all.35 = s16[8,354,256]{2,1,0:T(8,128)(2,1)S(1)} all-to-all(s16[8,354,256]{2,1,0:T(8,128)(2,1)S(1)} %pad_add_fusion.4), channel_id=1, replica_groups=mesh['dp'=4,'expert'=8] {'expert'}, dimensions={0} | all-to-all | bytes 2899968 | tf_op jit(solution)/shard_map/all_to_all | solution.py:63
  371.6 4.3 all-to-all-start.6
  378.7 32.9 %all-to-all-done.6 = s16[8,354,256]{2,1,0:T(8,128)(2,1)} async-done(((s16[8,354,256]{2,1,0:T(8,128)(2,1)}), s16[8,354,256]{2,1,0:T(8,128)(2,1)}, u32[]{:S(2)}, u32[]{:S(2)}) %all-to-all-start.6) | async-done | bytes 1450016 | tf_op jit(solution)/shard_map/all_to_all | solution.py:63
  411.6 4.5 all-to-all-start.5
  425.0 4.2 broadcast_in_dim_reshape.11
  429.2 22.4 %all-to-all-done.5 = s16[8,354,256]{2,1,0:T(8,128)(2,1)} async-done(((s16[8,354,256]{2,1,0:T(8,128)(2,1)}), s16[8,354,256]{2,1,0:T(8,128)(2,1)}, u32[]{:S(2)}, u32[]{:S(2)}) %all-to-all-start.5) | async-done | bytes 1450016 | tf_op jit(solution)/shard_map/all_to_all | solution.py:63
  457.5 4.2 broadcast_in_dim_reshape.10
  464.9 4.2 broadcast_in_dim_reshape.9
  469.1 6.3 %copy.63 = bf16[1,1408,2048]{2,1,0:T(8,128)(2,1)} copy(bf16[1,1408,2048]{2,1,0:T(8,128)(2,1)} %bitcast.109) | data formatting | bytes 11534336
  (100 shorter events, 74.9 us)
Async XLA Ops:
  8.0 1.9 copy-start
  8.0 190.5 %reduce-scatter.4.cloned.1.call-start = ((), (), s32[]{:S(2)}) async-start(), calls=%async_computation.10 | async-start | bytes 14417920
  34.9 1.0 copy-start.3
  34.9 1.0 copy-start.4
  34.9 254.3 %all-gather.6.cloned.1.call-start = ((), (), s32[]{:S(2)}) async-start(), calls=%async_computation.9 | async-start | bytes 17301504 | tf_op jit(solution)/shard_map/all_gather | solution.py:102
  43.5 53.3 %all-to-all-start.3 = ((s16[8,354,256]{2,1,0:T(8,128)(2,1)}), s16[8,354,256]{2,1,0:T(8,128)(2,1)}, u32[]{:S(2)}, u32[]{:S(2)}) async-start(s16[8,354,256]{2,1,0:T(8,128)(2,1)} %pad_add_fusion.3), calls=%async_computation.3 | async-start | bytes 2949120 | tf_op jit(solution)/shard_map/all_to_all | solution.py:63
  96.8 55.3 %all-to-all-start.1 = ((s16[8,354,256]{2,1,0:T(8,128)(2,1)}), s16[8,354,256]{2,1,0:T(8,128)(2,1)}, u32[]{:S(2)}, u32[]{:S(2)}) async-start(s16[8,354,256]{2,1,0:T(8,128)(2,1)} %pad_add_fusion.1), calls=%async_computation.1 | async-start | bytes 2949120 | tf_op jit(solution)/shard_map/all_to_all | solution.py:63
  152.1 76.2 %all-to-all-start = ((s16[8,354,256]{2,1,0:T(8,128)(2,1)}), s16[8,354,256]{2,1,0:T(8,128)(2,1)}, u32[]{:S(2)}, u32[]{:S(2)}) async-start(s16[8,354,256]{2,1,0:T(8,128)(2,1)} %pad_add_fusion), calls=%async_computation | async-start | bytes 2949120 | tf_op jit(solution)/shard_map/all_to_all | solution.py:63
  207.8 24.9 %copy-start.5 = (s32[8]{0:T(128)S(1)}, s32[8]{0:T(128)}, u32[]{:S(2)}) copy-start(s32[8]{0:T(128)} %param.25) | copy-start | bytes 100
  228.3 60.1 %all-to-all-start.2 = ((s16[8,354,256]{2,1,0:T(8,128)(2,1)}), s16[8,354,256]{2,1,0:T(8,128)(2,1)}, u32[]{:S(2)}, u32[]{:S(2)}) async-start(s16[8,354,256]{2,1,0:T(8,128)(2,1)} %pad_add_fusion.2), calls=%async_computation.2 | async-start | bytes 2949120 | tf_op jit(solution)/shard_map/all_to_all | solution.py:63
  232.6 236.5 %all-gather.4.cloned.1.call-start = ((), (), s32[]{:S(2)}) async-start(), calls=%async_computation.8 | async-start | bytes 7208960 | tf_op jit(solution)/shard_map/all_gather | solution.py:67
  296.2 10.6 %copy-start.2 = (f32[64,2048]{1,0:T(8,128)}, f32[64,2048]{1,0:T(8,128)S(1)}, u32[]{:S(2)}) copy-start(f32[64,2048]{1,0:T(8,128)S(1)} %reduce_sum.28) | copy-start | bytes 1572868
  371.6 40.0 %all-to-all-start.6 = ((s16[8,354,256]{2,1,0:T(8,128)(2,1)}), s16[8,354,256]{2,1,0:T(8,128)(2,1)}, u32[]{:S(2)}, u32[]{:S(2)}) async-start(s16[8,354,256]{2,1,0:T(8,128)(2,1)} %pad_add_fusion.6), calls=%async_computation.6 | async-start | bytes 2949120 | tf_op jit(solution)/shard_map/all_to_all | solution.py:63
  411.6 40.0 %all-to-all-start.5 = ((s16[8,354,256]{2,1,0:T(8,128)(2,1)}), s16[8,354,256]{2,1,0:T(8,128)(2,1)}, u32[]{:S(2)}, u32[]{:S(2)}) async-start(s16[8,354,256]{2,1,0:T(8,128)(2,1)} %pad_add_fusion.5), calls=%async_computation.5 | async-start | bytes 2949120 | tf_op jit(solution)/shard_map/all_to_all | solution.py:63
  469.1 6.3 %copy-start.1 = (bf16[1,1152,1408]{2,1,0:T(8,128)(2,1)S(1)}, bf16[1,1152,1408]{2,1,0:T(8,128)(2,1)}, u32[]{:S(2)}) copy-start(bf16[1,1152,1408]{2,1,0:T(8,128)(2,1)} %param.14) | copy-start | bytes 9732100
Sparse Core Ops, SparseCore 0:
  35.1 163.4 reduce-scatter.3
  369.1 64.6 all-gather.3
Sparse Core Ops, SparseCore 1:
  39.0 195.6 all-gather.5
